TPU v7x, 256 devices: a whole 4x4x8 slice. The times are simulated.
256 devices in a mesh: tile: 128 (over x, y_lo, z, core), trc: 2 (over y_hi).
Axes of the slice: x: 4, y: 4 (y_hi: 2, y_lo: 2; y = y_hi * 2 + y_lo), z: 8, core: 2. Of those that a mesh axis runs over, the one named last changes fastest.
Arguments:
- tracers: float32 [32, 47, 768, 256], P('trc', None, 'tile'), may hold values from -6 to 6
- courant: float32 [47, 768, 256], P(None, 'tile'), may hold values from -0.4 to 0.4
- vertical_mix: float32 [47, 768, 256], P(None, 'tile'), may hold values from 0.02 to 0.12
- kernel_profile: float32 [47], replicated, may hold values from 0.25 to 1.75
- obs_cell: int32 [262144], P('tile'), may hold values from 0 to 1535
- obs_top: int32 [262144], P('tile'), may hold values from 1 to 47
- obs_count: int32 [128], P('tile'), may hold values from 1 to 2048, 131072 in all
- innovation: float32 [262144], P('tile'), may hold values from -6 to 6
- obs_error: float32 [262144], P('tile'), may hold values from 0.3 to 3
- prior_precision: float32 [32], replicated, may hold values from 0.5 to 2
Outputs:
- fields: float32 [32, 47, 768, 256], P('trc', None, 'tile')
- update: float32 [32], replicated
- misfit: float32 [262144], P('tile')
Inputs may be any that keep to these rules, and one draw needn't show every extreme that they name: obs_cell counts cells of the observation's own tile. `obs_count`: the counts sum to 131072 and some tile is full.
All inputs are finite; a program needn't handle non-finite values. No bound on the sum of `obs_count` on one device may be relied on, other than what follows from the above.
Results may differ from a plain program's by a relative error of at most 0.0003.
Values sent between devices are 32-bit elements; how exact they have to be, the bound alone decides.
No kernel may reach another device: no remote copies, remote signals or barrier semaphores. Data moves between devices by JAX's collectives and lax.ppermute only.
A program may use at most 192 MiB of HBM per device.

v0:
```python
import functools

import jax
import jax.numpy as jnp
from jax import lax
from jax.sharding import Mesh
from jax.sharding import PartitionSpec as P

STEPS = 3
TILE = ("tile_0", "tile_1", "tile_2", "tile_3")


HORIZ = 0.05


def shifted(shard, axis, by):
    length = lax.axis_size(axis)
    return lax.ppermute(shard, axis, [(i, (i + by) % length) for i in range(length)])


def padded_2(shard, sides, width):
    for axis, dim in sides:
        size, length = (lax.axis_size(axis), shard.shape[dim])
        up = [(i, (i + 1) % size) for i in range(size)]
        down = [(j, i) for i, j in up]
        last = lax.slice_in_dim(shard, length - width, length, axis=dim)
        leading = lax.slice_in_dim(shard, 0, width, axis=dim)
        before = lax.ppermute(last, axis, up)
        after = lax.ppermute(leading, axis, down)
        shard = jnp.concatenate([before, shard, after], axis=dim)
    return shard


def from_everyone(shard, axis):
    length = lax.axis_size(axis)
    return lax.all_to_all(
        jnp.broadcast_to(shard[None], (length, *shard.shape)), axis, 0, 0, tiled=True
    )


def joined_along(blocks, dim):
    blocks = jnp.moveaxis(blocks, 0, dim)
    dims = blocks.shape
    return blocks.reshape(*dims[:dim], dims[dim] * dims[dim + 1], *dims[dim + 2 :])


def gathered_copies(shard, axis, dim):
    blocks = from_everyone(shard, axis)
    return joined_along(blocks, dim)


def by_axis(shard, axes):
    return functools.reduce(lax.psum, axes, shard)


def advance(padded, wind_pad, mix_pad):
    centre = padded[:, :, 1:-1]
    left = padded[:, :, :-2]
    right = padded[:, :, 2:]
    wind_here = wind_pad[:, 1:-1]
    wind_east = wind_pad[:, 2:]
    mixing = mix_pad[:, 1:-1]
    inflow = jnp.maximum(wind_here, 0.0) * left + jnp.minimum(wind_here, 0.0) * centre
    outflow = jnp.maximum(wind_east, 0.0) * centre + jnp.minimum(wind_east, 0.0) * right
    north = jnp.concatenate([centre[..., 1:], centre[..., -1:]], -1)
    south = jnp.concatenate([centre[..., :1], centre[..., :-1]], -1)
    above = jnp.concatenate([centre[:, 1:], centre[:, -1:]], 1)
    below = jnp.concatenate([centre[:, :1], centre[:, :-1]], 1)
    return (
        centre
        + inflow
        - outflow
        + HORIZ * (left + right - 2.0 * centre)
        + HORIZ * (north + south - 2.0 * centre)
        + mixing * (above + below - 2.0 * centre)
    )


def per_device(
    tracers,
    courant,
    vertical_mix,
    kernel_profile,
    obs_cell,
    obs_top,
    obs_count,
    innovation,
    obs_error,
    prior_precision,
):
    fields = tracers
    east_wind = shifted(courant[:, :1, :], TILE, -1)
    blank = jnp.zeros_like(courant[:, :1, :])
    wind_pad = jnp.concatenate([blank, courant, east_wind], 1)
    mix_pad = jnp.concatenate([blank, vertical_mix, blank], 1)
    for step in range(STEPS):
        padded = padded_2(fields, ((TILE, 2),), 1)
        fields = advance(padded, wind_pad, mix_pad)
    groups, levels_n, columns, rows_lat = fields.shape
    flat = fields.reshape(groups, levels_n, columns * rows_lat)
    values = flat[:, :, obs_cell]
    levels = jnp.arange(levels_n, dtype=jnp.int32)
    weights = kernel_profile[:, None] * (levels[:, None] < obs_top[None, :]).astype(jnp.float32)
    mine = jnp.einsum("tlk,lk->tk", values, weights, precision=lax.Precision.HIGHEST)
    jacobian = gathered_copies(mine, "trc", 0)
    slots = jnp.arange(obs_cell.shape[0], dtype=jnp.int32)
    live = (slots < obs_count[0]).astype(jnp.float32)
    weight = live / obs_error
    weighted = jacobian * weight[None, :]
    gram_part = jnp.dot(weighted, jacobian.T, precision=lax.Precision.HIGHEST)
    grad_part = jnp.dot(weighted, innovation, precision=lax.Precision.HIGHEST)
    gram_sum, gradient = (by_axis(gram_part, TILE), by_axis(grad_part, TILE))
    gram = gram_sum + jnp.diag(prior_precision)
    factor = jnp.linalg.cholesky(gram)
    update = jax.scipy.linalg.cho_solve((factor, True), gradient)
    fitted = jnp.dot(update, jacobian, precision=lax.Precision.HIGHEST)
    misfit = live * (innovation - fitted)
    return (fields, update, misfit)


def solution(mesh):
    split = Mesh(
        mesh.devices.reshape(4, 2, 8, 2, mesh.shape["trc"]),
        ("tile_0", "tile_1", "tile_2", "tile_3", "trc"),
    )
    return jax.shard_map(
        per_device,
        mesh=split,
        in_specs=(
            P("trc", None, TILE, None),
            P(None, TILE, None),
            P(None, TILE, None),
            P(),
            P(TILE),
            P(TILE),
            P(TILE),
            P(TILE),
            P(TILE),
            P(),
        ),
        out_specs=(P("trc", None, TILE, None), P(), P(TILE)),
        check_vma=False,
    )
```

profile of v0, /device:TPU:1, one launch (start us, length us, event | category | flops | bytes accessed | tf_op | source)
XLA Modules:
  0.0 260.8 jit_solution(11222104191724720827)
XLA Ops:
  0.6 1.4 slice.143
  2.0 3.2 %collective-permute-start.1 = (f32[47,1,256]{2,0,1:T(8,128)}, f32[47,1,256]{2,0,1:T(8,128)S(1)}, u32[]{:S(2)}, u32[]{:S(2)}) collective-permute-start(f32[47,1,256]{2,0,1:T(8,128)} %slice.143), channel_id=1, source_target_pairs={{0,254},{2,0},{4,2},{6,4},{8,6},{10,8},{12,10},{14,12},{16,14},{18... | collective-permute-start | bytes 144392 | tf_op jit(solution)/shard_map/ppermute | solution.py:18
  5.3 2.6 %fusion.43 = (f32[16,47,1,256]{3,0,2,1:T(8,128)}, f32[16,47,1,256]{3,0,2,1:T(8,128)}) fusion(f32[16,47,6,256]{3,0,2,1:T(8,128)} %param.10), kind=kLoop, calls=%fused_computation.75 | loop fusion | bytes 3080192 | tf_op jit(solution)/shard_map/slice | solution.py:26
  7.9 6.9 %collective-permute-start.2 = (f32[16,47,1,256]{3,0,2,1:T(8,128)}, f32[16,47,1,256]{3,0,2,1:T(8,128)}, u32[]{:S(2)}, u32[]{:S(2)}) collective-permute-start(f32[16,47,1,256]{3,0,2,1:T(8,128)} %get-tuple-element.32), channel_id=1, source_target_pairs={{2,0},{4,2},{6,4},{8,6},{10,8},{12,10},{14,12},{16,14},{18,16},{20... | collective-permute-start | bytes 2310152 | tf_op jit(solution)/shard_map/ppermute | solution.py:29
  14.8 8.8 %fusion.47 = (f32[16,47,6,255]{3,0,2,1:T(8,128)}, f32[16,47,6,255]{3,0,2,1:T(8,128)}) fusion(f32[16,47,6,256]{3,0,2,1:T(8,128)} %param.10), kind=kLoop, calls=%fused_computation.79 | loop fusion | bytes 18408960 | tf_op jit(solution)/shard_map/slice | solution.py:66
  23.6 4.7 %fusion.45 = (f32[16,46,6,256]{3,0,2,1:T(8,128)}, f32[16,46,6,256]{3,0,2,1:T(8,128)}) fusion(f32[16,47,6,256]{3,0,2,1:T(8,128)S(1)} %bitcast.47), kind=kLoop, calls=%fused_computation.77 | loop fusion | bytes 18087936 | tf_op jit(solution)/shard_map/slice | solution.py:68
  28.5 2.2 fusion.46
  30.7 0.6 fusion.44
  31.4 0.2 copy.24
  31.6 1.9 copy.29
  34.3 1.2 fusion.21
  35.5 0.2 copy.20
  35.6 0.2 copy.21
  35.8 0.2 copy.22
  36.3 14.5 %fusion.5 = f32[16,47,6,256]{3,0,2,1:T(8,128)S(1)} fusion(f32[16,47,6,1]{3,0,2,1:T(8,128)S(1)} %copy-done, f32[16,47,6,255]{3,0,2,1:T(8,128)} %get-tuple-element.40, f32[16,47,6,255]{3,0,2,1:T(8,128)} %get-tuple-element.39, f32[16,47,6,1]{3,0,2,1:T(8,128)S(1)} %get-tuple-element.37, f32[16,1,6,256]{3,0,2,1:T(8,128)} %get-tuple-element.34, ...), kind=kLoop, calls=%fused_computation.13 | loop fusion | flops 31186944 | bytes 30705664 | tf_op jit(solution)/shard_map/add | solution.py:70
  50.8 4.7 %fusion.40 = (f32[16,46,6,256]{3,0,2,1:T(8,128)}, f32[16,46,6,256]{3,0,2,1:T(8,128)}) fusion(f32[16,47,6,256]{3,0,2,1:T(8,128)S(1)} %fusion.5), kind=kLoop, calls=%fused_computation.72 | loop fusion | bytes 18087936 | tf_op jit(solution)/shard_map/slice | solution.py:68
  55.5 3.0 %fusion.41 = (f32[16,47,6,1]{3,0,2,1:T(8,128)}, f32[16,47,6,1]{3,0,2,1:T(8,128)}) fusion(f32[16,47,6,256]{3,0,2,1:T(8,128)S(1)} %fusion.5), kind=kLoop, calls=%fused_computation.73 | loop fusion | bytes 72192 | tf_op jit(solution)/shard_map/slice | solution.py:66
  58.8 6.1 %collective-permute-start.4 = (f32[16,47,1,256]{3,0,2,1:T(8,128)S(1)}, f32[16,47,1,256]{3,0,2,1:T(8,128)S(1)}, u32[]{:S(2)}, u32[]{:S(2)}) collective-permute-start(f32[16,47,1,256]{3,0,2,1:T(8,128)S(1)} %get-tuple-element.22), channel_id=1, source_target_pairs={{2,0},{4,2},{6,4},{8,6},{10,8},{12,10},{14,12},{16,14},{18,16},{20... | collective-permute-start | bytes 2310152 | tf_op jit(solution)/shard_map/ppermute | solution.py:29
  64.9 0.7 fusion.39
  65.6 1.9 fusion.42
  67.6 2.7 %collective-permute-done.4 = f32[16,47,1,256]{3,0,2,1:T(8,128)S(1)} collective-permute-done((f32[16,47,1,256]{3,0,2,1:T(8,128)S(1)}, f32[16,47,1,256]{3,0,2,1:T(8,128)S(1)}, u32[]{:S(2)}, u32[]{:S(2)}) %collective-permute-start.4) | collective-permute-done | bytes 770080 | tf_op jit(solution)/shard_map/ppermute | solution.py:29
  70.3 0.9 copy-done.6
  71.2 9.9 %fusion.11 = f32[16,47,6,256]{3,0,2,1:T(8,128)S(1)} fusion(f32[16,47,6,1]{3,0,2,1:T(8,128)} %get-tuple-element.28, f32[16,47,6,255]{3,0,2,1:T(8,128)S(1)} %get-tuple-element.30, f32[16,47,6,255]{3,0,2,1:T(8,128)S(1)} %get-tuple-element.29, f32[16,47,6,1]{3,0,2,1:T(8,128)} %get-tuple-element.27, f32[16,1,6,256]{3,0,2,1:T(8,128)} %get-tuple-element.24, ...), kind=kLoop, calls=%fused_computation.21 | loop fusion | flops 31186944 | bytes 30705664 | tf_op jit(solution)/shard_map/add | solution.py:70
  81.1 2.9 %fusion.35 = (f32[16,46,6,256]{3,0,2,1:T(8,128)S(1)}, f32[16,46,6,256]{3,0,2,1:T(8,128)}) fusion(f32[16,47,6,256]{3,0,2,1:T(8,128)S(1)} %fusion.11), kind=kLoop, calls=%fused_computation.67 | loop fusion | bytes 18087936 | tf_op jit(solution)/shard_map/slice | solution.py:68
  84.0 3.0 %fusion.36 = (f32[16,47,6,1]{3,0,2,1:T(8,128)}, f32[16,47,6,1]{3,0,2,1:T(8,128)}) fusion(f32[16,47,6,256]{3,0,2,1:T(8,128)S(1)} %fusion.11), kind=kLoop, calls=%fused_computation.68 | loop fusion | bytes 72192 | tf_op jit(solution)/shard_map/slice | solution.py:66
  87.0 1.3 fusion.33
  88.3 10.1 %collective-permute-start.6 = (f32[16,47,1,256]{3,0,2,1:T(8,128)}, f32[16,47,1,256]{3,0,2,1:T(8,128)}, u32[]{:S(2)}, u32[]{:S(2)}) collective-permute-start(f32[16,47,1,256]{3,0,2,1:T(8,128)} %get-tuple-element.12), channel_id=1, source_target_pairs={{2,0},{4,2},{6,4},{8,6},{10,8},{12,10},{14,12},{16,14},{18,16},{20... | collective-permute-start | bytes 2310152 | tf_op jit(solution)/shard_map/ppermute | solution.py:29
  98.4 1.9 fusion.37
  100.6 10.7 %fusion.17 = f32[16,47,6,256]{3,0,2,1:T(8,128)} fusion(f32[16,47,6,1]{3,0,2,1:T(8,128)} %get-tuple-element.18, f32[16,47,6,255]{3,0,2,1:T(8,128)S(1)} %get-tuple-element.20, f32[16,47,6,255]{3,0,2,1:T(8,128)S(1)} %get-tuple-element.19, f32[16,47,6,1]{3,0,2,1:T(8,128)} %get-tuple-element.17, f32[16,1,6,256]{3,0,2,1:T(8,128)S(1)} %get-tuple-element.14, ...), kind=kLoop, calls=%fused_computation.29 | loop fusion | flops 31186944 | bytes 30705664 | tf_op jit(solution)/shard_map/add | solution.py:70
  111.3 11.1 %copy.31 = f32[16,47,6,256]{1,0,3,2:T(8,128)} copy(f32[16,47,6,256]{3,0,2,1:T(8,128)} %fusion.17) | data formatting | bytes 9240576 | tf_op jit(solution)/shard_map/reshape | solution.py:100
  122.4 23.5 %gather_fusion = f32[2048,16,47]{2,1,0:T(8,128)} fusion(f32[16,47,1536]{1,0,2:T(8,128)} %bitcast.48, s32[2048]{0:T(1024)S(1)} %fusion.29), kind=kCustom, calls=%fused_computation | custom fusion | bytes 12328960 | tf_op jit(solution)/shard_map/gather | solution.py:101
  146.0 29.0 %fusion = f32[2048,1,16]{2,1,0:T(1,128)S(1)} fusion(f32[47,2048,1]{0,2,1:T(1,128)S(1)} %copy-done.4, f32[2048,16,47]{2,1,0:T(8,128)} %gather_fusion), kind=kOutput, calls=%fused_computation.1 | convolution fusion | flops 18481152 | bytes 6676480 | tf_op jit(solution)/shard_map/tlk,lk->tk/dot_general | solution.py:104
  174.9 0.3 copy.27
  175.2 0.7 broadcast_in_dim.20
  176.0 3.9 %all-to-all-start = ((f32[2,16,2048]{2,1,0:T(8,128)}), f32[2,16,2048]{2,1,0:T(8,128)S(1)}, u32[]{:S(2)}, u32[]{:S(2)}) async-start(f32[2,16,2048]{2,1,0:T(8,128)} %broadcast_in_dim.20), calls=%async_computation | async-start | bytes 524288 | tf_op jit(solution)/shard_map/all_to_all | solution.py:36
  179.9 5.5 %all-to-all-done = f32[2,16,2048]{2,1,0:T(8,128)S(1)} async-done(((f32[2,16,2048]{2,1,0:T(8,128)}), f32[2,16,2048]{2,1,0:T(8,128)S(1)}, u32[]{:S(2)}, u32[]{:S(2)}) %all-to-all-start) | async-done | bytes 262176 | tf_op jit(solution)/shard_map/all_to_all | solution.py:36
  185.4 0.3 fusion.48
  185.8 0.3 convolution_bitcast_fusion.1
  186.0 11.3 %all-reduce.1 = (f32[32,32]{1,0:T(8,128)S(1)}, f32[32]{0:T(128)S(1)}) all-reduce(f32[32,32]{1,0:T(8,128)S(1)} %fusion.48, f32[32]{0:T(128)S(1)} %convolution_bitcast_fusion.1), channel_id=1, replica_groups=mesh['tile_0'=4,'tile_1'=2,'tile_2'=8,'tile_3'=2,'trc'=2] {'tile_0'}, use_global_device_ids=true, to_apply=%region_0.0 | all-reduce | flops 1056 | bytes 8448 | tf_op jit(solution)/shard_map/psum | solution.py:53
  197.3 5.1 %all-reduce.3 = (f32[32,32]{1,0:T(8,128)S(1)}, f32[32]{0:T(128)S(1)}) all-reduce(f32[32,32]{1,0:T(8,128)S(1)} %get-tuple-element.5, f32[32]{0:T(128)S(1)} %get-tuple-element.6), channel_id=1, replica_groups=mesh['tile_0'=4,'tile_1'=2,'tile_2'=8,'tile_3'=2,'trc'=2] {'tile_1'}, use_global_device_ids=true, to_apply=%region_1.0 | all-reduce | flops 1056 | bytes 8448 | tf_op jit(solution)/shard_map/psum | solution.py:53
  202.4 38.6 %all-reduce = (f32[32,32]{1,0:T(8,128)S(1)}, f32[32]{0:T(128)S(1)}) all-reduce(f32[32,32]{1,0:T(8,128)S(1)} %get-tuple-element.9, f32[32]{0:T(128)S(1)} %get-tuple-element.10), channel_id=1, replica_groups=mesh['tile_0'=4,'tile_1'=2,'tile_2'=8,'tile_3'=2,'trc'=2] {'tile_2'}, use_global_device_ids=true, to_apply=%region_2.0 | all-reduce | flops 1056 | bytes 8448 | tf_op jit(solution)/shard_map/psum | solution.py:53
  241.0 11.6 %all-reduce.2 = (f32[32,32]{1,0:T(8,128)S(1)}, f32[32]{0:T(128)S(1)}) all-reduce(f32[32,32]{1,0:T(8,128)S(1)} %get-tuple-element.3, f32[32]{0:T(128)S(1)} %get-tuple-element.4), channel_id=1, replica_groups=mesh['tile_0'=4,'tile_1'=2,'tile_2'=8,'tile_3'=2,'trc'=2] {'tile_3'}, use_global_device_ids=true, to_apply=%region_3.0 | all-reduce | flops 1056 | bytes 8448 | tf_op jit(solution)/shard_map/psum | solution.py:53
  252.9 2.9 %cholesky.16 = f32[32,32]{1,0:T(8,128)S(1)} custom-call(f32[32,32]{1,0:T(8,128)S(1)} %fusion.28), custom_call_target="Cholesky" | custom-call | tf_op jit(solution)/shard_map/jit(cholesky)/cholesky | solution.py:114
  255.8 0.6 compare_reduce_fusion
  256.5 0.7 fusion.24
  257.1 2.4 custom-call.10
  259.9 0.3 fusion.30
  260.2 0.6 subtract_select_fusion
  (56 shorter events, 1.5 us)
Async XLA Ops:
  2.0 32.2 %collective-permute-start.1 = (f32[47,1,256]{2,0,1:T(8,128)}, f32[47,1,256]{2,0,1:T(8,128)S(1)}, u32[]{:S(2)}, u32[]{:S(2)}) collective-permute-start(f32[47,1,256]{2,0,1:T(8,128)} %slice.143), channel_id=1, source_target_pairs={{0,254},{2,0},{4,2},{6,4},{8,6},{10,8},{12,10},{14,12},{16,14},{18... | collective-permute-start | bytes 144392 | tf_op jit(solution)/shard_map/ppermute | solution.py:18
  7.9 28.3 %collective-permute-start = (f32[16,47,1,256]{3,0,2,1:T(8,128)}, f32[16,47,1,256]{3,0,2,1:T(8,128)}, u32[]{:S(2)}, u32[]{:S(2)}) collective-permute-start(f32[16,47,1,256]{3,0,2,1:T(8,128)} %get-tuple-element.31), channel_id=1, source_target_pairs={{0,2},{2,4},{4,6},{6,8},{8,10},{10,12},{12,14},{14,16},{16,18},{18... | collective-permute-start | bytes 2310152 | tf_op jit(solution)/shard_map/ppermute | solution.py:28
  7.9 15.7 %slice-start = ((s8[4620288]{0:T(1024)(128)(4,1)}), s8[4194304]{0:T(1024)(128)(4,1)S(1)}, s32[]{:S(2)}) async-start(s8[4620288]{0:T(1024)(128)(4,1)} %bitcast.46), calls=%async_computation.1 | async-start | bytes 8388608
  7.9 15.7 %slice-start.1 = ((s8[4620288]{0:T(1024)(128)(4,1)}), s8[425984]{0:T(1024)(128)(4,1)S(1)}, s32[]{:S(2)}) async-start(s8[4620288]{0:T(1024)(128)(4,1)} %bitcast.46), calls=%async_computation.2 | async-start | bytes 851968
  7.9 28.3 %collective-permute-start.2 = (f32[16,47,1,256]{3,0,2,1:T(8,128)}, f32[16,47,1,256]{3,0,2,1:T(8,128)}, u32[]{:S(2)}, u32[]{:S(2)}) collective-permute-start(f32[16,47,1,256]{3,0,2,1:T(8,128)} %get-tuple-element.32), channel_id=1, source_target_pairs={{2,0},{4,2},{6,4},{8,6},{10,8},{12,10},{14,12},{16,14},{18,16},{20... | collective-permute-start | bytes 2310152 | tf_op jit(solution)/shard_map/ppermute | solution.py:29
  23.6 4.8 %copy-start.9 = (s32[2048]{0:T(1024)S(1)}, s32[2048]{0:T(1024)}, u32[]{:S(2)}) copy-start(s32[2048]{0:T(1024)} %param.15) | copy-start | bytes 24580
  23.6 4.7 %copy-start.14 = (f32[47]{0:T(128)S(1)}, f32[47]{0:T(128)}, u32[]{:S(2)}) copy-start(f32[47]{0:T(128)} %param.13) | copy-start | bytes 568
  28.5 2.9 %copy-start.10 = (s32[2048]{0:T(1024)S(1)}, s32[2048]{0:T(1024)}, u32[]{:S(2)}) copy-start(s32[2048]{0:T(1024)} %param.14) | copy-start | bytes 24580
  28.5 2.9 %copy-start.7 = (f32[47,6,256]{2,0,1:T(8,128)S(1)}, f32[47,6,256]{2,0,1:T(8,128)}, u32[]{:S(2)}) copy-start(f32[47,6,256]{2,0,1:T(8,128)} %param.12) | copy-start | bytes 866308
  33.5 2.8 %copy-start = (f32[16,47,6,1]{3,0,2,1:T(8,128)S(1)}, f32[16,47,6,1]{3,0,2,1:T(8,128)}, u32[]{:S(2)}) copy-start(f32[16,47,6,1]{3,0,2,1:T(8,128)} %get-tuple-element.38) | copy-start | bytes 54148
  35.8 14.9 %copy-start.1 = (f32[47,6,256]{2,1,0:T(8,128)}, f32[47,6,256]{2,1,0:T(8,128)S(1)}, u32[]{:S(2)}) copy-start(f32[47,6,256]{2,1,0:T(8,128)S(1)} %copy.21) | copy-start | bytes 866308
  36.0 14.8 %copy-start.2 = (f32[47,6,256]{2,1,0:T(8,128)}, f32[47,6,256]{2,1,0:T(8,128)S(1)}, u32[]{:S(2)}) copy-start(f32[47,6,256]{2,1,0:T(8,128)S(1)} %copy.22) | copy-start | bytes 866308
  36.2 14.6 %copy-start.3 = (f32[47,6,256]{2,1,0:T(8,128)}, f32[47,6,256]{2,1,0:T(8,128)S(1)}, u32[]{:S(2)}) copy-start(f32[47,6,256]{2,1,0:T(8,128)S(1)} %copy.23) | copy-start | bytes 866308
  58.7 8.8 %collective-permute-start.3 = (f32[16,47,1,256]{3,0,2,1:T(8,128)S(1)}, f32[16,47,1,256]{3,0,2,1:T(8,128)S(1)}, u32[]{:S(2)}, u32[]{:S(2)}) collective-permute-start(f32[16,47,1,256]{3,0,2,1:T(8,128)S(1)} %get-tuple-element.21), channel_id=1, source_target_pairs={{0,2},{2,4},{4,6},{6,8},{8,10},{10,12},{12,14},{14,16},{16,18},{18... | collective-permute-start | bytes 2310152 | tf_op jit(solution)/shard_map/ppermute | solution.py:28
  58.8 11.5 %collective-permute-start.4 = (f32[16,47,1,256]{3,0,2,1:T(8,128)S(1)}, f32[16,47,1,256]{3,0,2,1:T(8,128)S(1)}, u32[]{:S(2)}, u32[]{:S(2)}) collective-permute-start(f32[16,47,1,256]{3,0,2,1:T(8,128)S(1)} %get-tuple-element.22), channel_id=1, source_target_pairs={{2,0},{4,2},{6,4},{8,6},{10,8},{12,10},{14,12},{16,14},{18,16},{20... | collective-permute-start | bytes 2310152 | tf_op jit(solution)/shard_map/ppermute | solution.py:29
  67.6 2.8 %copy-start.5 = (f32[16,47,1,256]{3,0,2,1:T(8,128)}, f32[16,47,1,256]{3,0,2,1:T(8,128)S(1)}, u32[]{:S(2)}) copy-start(f32[16,47,1,256]{3,0,2,1:T(8,128)S(1)} %collective-permute-done.3) | copy-start | bytes 2310148
  70.3 0.9 copy-start.6
  88.3 12.2 %collective-permute-start.5 = (f32[16,47,1,256]{3,0,2,1:T(8,128)}, f32[16,47,1,256]{3,0,2,1:T(8,128)}, u32[]{:S(2)}, u32[]{:S(2)}) collective-permute-start(f32[16,47,1,256]{3,0,2,1:T(8,128)} %get-tuple-element.11), channel_id=1, source_target_pairs={{0,2},{2,4},{4,6},{6,8},{8,10},{10,12},{12,14},{14,16},{16,18},{18... | collective-permute-start | bytes 2310152 | tf_op jit(solution)/shard_map/ppermute | solution.py:28
  88.3 12.3 %collective-permute-start.6 = (f32[16,47,1,256]{3,0,2,1:T(8,128)}, f32[16,47,1,256]{3,0,2,1:T(8,128)}, u32[]{:S(2)}, u32[]{:S(2)}) collective-permute-start(f32[16,47,1,256]{3,0,2,1:T(8,128)} %get-tuple-element.12), channel_id=1, source_target_pairs={{2,0},{4,2},{6,4},{8,6},{10,8},{12,10},{14,12},{16,14},{18,16},{20... | collective-permute-start | bytes 2310152 | tf_op jit(solution)/shard_map/ppermute | solution.py:29
  122.4 23.5 %copy-start.4 = (f32[47,2048,1]{0,2,1:T(1,128)S(1)}, f32[47,2048,1]{0,2,1:T(1,128)}, u32[]{:S(2)}) copy-start(f32[47,2048,1]{0,2,1:T(1,128)} %copy.29) | copy-start | bytes 1155076
  146.0 33.9 %copy-start.11 = (f32[2048]{0:T(1024)S(1)}, f32[2048]{0:T(1024)}, u32[]{:S(2)}) copy-start(f32[2048]{0:T(1024)} %param.18) | copy-start | bytes 24580
  146.0 39.8 %copy-start.8 = (f32[2048]{0:T(1024)S(1)}, f32[2048]{0:T(1024)}, u32[]{:S(2)}) copy-start(f32[2048]{0:T(1024)} %param.17) | copy-start | bytes 24580
  146.0 106.7 %copy-start.12 = (f32[32]{0:T(128)S(1)}, f32[32]{0:T(128)}, u32[]{:S(2)}) copy-start(f32[32]{0:T(128)} %param.19) | copy-start | bytes 388
  176.0 9.4 %all-to-all-start = ((f32[2,16,2048]{2,1,0:T(8,128)}), f32[2,16,2048]{2,1,0:T(8,128)S(1)}, u32[]{:S(2)}, u32[]{:S(2)}) async-start(f32[2,16,2048]{2,1,0:T(8,128)} %broadcast_in_dim.20), calls=%async_computation | async-start | bytes 524288 | tf_op jit(solution)/shard_map/all_to_all | solution.py:36
  259.9 0.9 copy-start.13
where the time goes:
time: 261 us
  local copies, waits for them, and re-layouts  79.6 us (30%)
  blocking collectives  66.6 us (26%)
  other arithmetic  43.8 us (17%)
  starting transfers between devices  30.3 us (12%)
  matrix products  30.1 us (12%)
  waiting for transfers between devices  8.56 us (3%)
    psum x4, blocking collectives, by_axis(): return functools.reduce(lax.psum, axes, shard)  66.6 us
    add x3, other arithmetic, advance(): centre + inflow - outflow + HORIZ * (left + right - 2.0 * centre)  35.1 us
    dot_general x1, matrix products, per_device(): jnp.einsum('tlk,lk->tk', values, weights, precision=lax.Precision.HIGHEST)  29 us
    gather x1, local copies, waits for them, and re-layouts, per_device(): values = flat[:, :, obs_cell]  23.5 us
    ppermute x3, starting transfers between devices, padded_2(): after = lax.ppermute(leading, axis, down)  23.1 us
    slice x6, local copies, waits for them, and re-layouts, advance(): south = jnp.concatenate([centre[..., :1], centre[..., :-1]], -1)  21 us
    slice x6, local copies, waits for them, and re-layouts, advance(): below = jnp.concatenate([centre[:, :1], centre[:, :-1]], 1)  13.7 us
    reshape x1, local copies, waits for them, and re-layouts, per_device(): flat = fields.reshape(groups, levels_n, columns * rows_lat)  11.1 us
  transfers between devices with their start and end apart: 8, of which 4 were waited for; matrix products, arithmetic and copies ran while one was open for 11% of the time, Pallas kernels for 0%

commit v1 on v0

v1 whole, which is shorter than its diff:
```python
import jax
import jax.numpy as jnp
from jax import lax
from jax.experimental import pallas as pl
from jax.experimental.pallas import tpu as pltpu
from jax.sharding import Mesh
from jax.sharding import PartitionSpec as P

TILE = ("tile_0", "tile_1", "tile_2", "tile_3")
HORIZ = 0.05
LEV = 47
LEVELS = 48
TR = 16
LAT = 256
OBS = 2048
ROWS = 6 * LAT
F32 = jnp.float32
EXACT = lax.Precision.HIGHEST
GROUPS = ((0, 1),)


def own(core, p):
    return p + core * (5 - 2 * p)


def triple(core, q):
    return q + core * (2 - 2 * q)


def coefficients(core, faces, mixes, cells, cm, cp, cd):
    sign = (1 - 2 * core).astype(F32)

    def wind(p):
        return faces[p + 3 + core * (6 - 2 * p)] * sign

    for j, p in enumerate(cells):
        here, there = wind(p), wind(p + 1)
        cm[j] = jnp.maximum(here, 0.0) + HORIZ
        cp[j] = HORIZ - jnp.minimum(there, 0.0)
        mixing = mixes[own(core, p) + 2]
        cd[j] = (1.0 - 4.0 * HORIZ) + jnp.minimum(here, 0.0) - jnp.maximum(there, 0.0) - 2.0 * mixing


def across(halves, start, end):
    low, high = halves
    ahead, back = [pltpu.roll(x, 127, 1) for x in halves], [pltpu.roll(x, 1, 1) for x in halves]
    north = [jnp.where(end, ahead[1], ahead[0]), jnp.where(end, high, ahead[1])]
    south = [jnp.where(start, low, back[0]), jnp.where(start, back[0], back[1])]
    return [HORIZ * (n + s) for n, s in zip(north, south)]


def march(core, groups, cells, first, source, mixes, cm, cp, cd, emit, extra=(), unroll=8):
    lane = lax.broadcasted_iota(jnp.int32, (8, 128), 1)
    start, end = lane == 0, lane == 127
    pairs_of = [(p, g) for p in cells for g in groups]

    def load(l, p, g):
        ref, index = source(l, p)
        return [ref[(*index, pl.ds(8 * g, 8), pl.ds(128 * h, 128))] for h in (0, 1)]

    def one(level, state):
        below, here, sides, more = state
        up = jnp.minimum(level + 1, LEV - 1)
        above = {k: load(up, *k) for k in pairs_of}
        beyond = {k: across(above[k], start, end) for k in pairs_of}
        rows = {}
        for p in cells:
            row = pl.ds(level, 1)
            j, mix_at = p - first, own(core, p) + 2
            rows[p] = [jnp.broadcast_to(ref[k, row, :], (8, LAT)) for ref, k in ((cd, j), (cm, j), (cp, j), (mixes, mix_at))]
        for p, g in pairs_of:
            minus = here[p - 1, g] if p - 1 in cells else load(jnp.minimum(level, LEV - 1), p - 1, g)
            plus = here[p + 1, g] if p + 1 in cells else load(jnp.minimum(level, LEV - 1), p + 1, g)
            for h in (0, 1):
                d, m, q, mixing = (x[:, 128 * h : 128 * h + 128] for x in rows[p])
                new = (d * here[p, g][h] + sides[p, g][h]) + (m * minus[h] + q * plus[h])
                new = new + mixing * (above[p, g][h] + below[p, g][h])
                more = emit(level, p, g, h, new, more)
        return here, above, beyond, more

    def body(i, state):
        for u in range(unroll):
            state = one(i * unroll + u, state)
        return state

    bottom = {k: load(0, *k) for k in pairs_of}
    lax.fori_loop(0, LEVELS // unroll, body, (bottom, bottom, {k: across(bottom[k], start, end) for k in pairs_of}, extra))


def storing(target):
    def emit(level, p, g, h, new, more):
        ref, at = target(level, p)
        ref[(*at, pl.ds(8 * g, 8), pl.ds(128 * h, 128))] = new
        return more

    return emit


def transposed_rows(prefix, table, place):
    for q in range(3):
        for group in range(6):
            for h in (0, 1):
                block = prefix[pl.ds(8 * group, 8), q, :, pl.ds(128 * h, 128)].reshape(128, 128)
                table[pl.ds(place(q) + group * LAT + 128 * h, 128), :] = block.T


def final_step(core, groups, cells, first, source, mixes, cm, cp, cd, kp, slot, done, prefix):
    zero = jnp.zeros((8, 128), F32)

    def emit(level, p, g, h, new, sums):
        at = (level, slot(p), pl.ds(8 * g, 8), pl.ds(128 * h, 128))
        done[at] = new
        total = sums[p, g, h] + kp[level] * new
        prefix[at] = total
        return {**sums, (p, g, h): total}

    sums = {(p, g, h): zero for p in cells for g in groups for h in (0, 1)}
    march(core, groups, cells, first, source, mixes, cm, cp, cd, emit, sums)


def edge_kernel(side_ref, cells, out, sems):
    copies = []
    for k in range(4):
        levels = pl.ds(12 * k, min(12, LEV - 12 * k))
        copies.append(pltpu.make_async_copy(cells.at[levels, pl.ds(3 * side_ref[0], 3)], out.at[levels], sems.at[k]))
    for copy in copies:
        copy.start()
    for copy in copies:
        copy.wait()


def early_kernel(core_ref, kp, cells_hbm, halo, wind, mix, wind_mix_halo, out, carry, table, faces, mixes, tracers, cm, cp, cd, s1, s2, done, prefix, sem, sems):
    core = core_ref[0]
    loads = [pltpu.make_async_copy(cells_hbm.at[pl.ds(12 * k, min(12, LEV - 12 * k))], tracers.at[pl.ds(12 * k, min(12, LEV - 12 * k))], sems.at[k]) for k in range(4)]
    for load in loads:
        load.start()
    faces[3:9, :LEV] = wind[...]
    faces[pl.ds(9 - 9 * core, 3), :LEV] = wind_mix_halo[0:3]
    mixes[2:8, :LEV] = mix[...]
    mixes[pl.ds(8 - 8 * core, 2), :LEV] = wind_mix_halo[3:5]
    cells = range(1, 8)
    coefficients(core, faces, mixes, cells, cm, cp, cd)

    def source0(l, p):
        return (tracers, (l, own(core, p))) if p < 6 else (halo, (l, triple(core, p - 6)))

    def source1(l, p):
        return (carry, (l, p + 1)) if p < 3 else (s1, (l, p - 3))

    def source2(l, p):
        return (carry, (l, p + 2)) if p < 4 else (s2, (l, p - 4))

    for load in loads:
        load.wait()

    def keep(level, _):
        carry[level, 0] = tracers[level, own(core, 0)]
        carry[level, 1] = tracers[level, own(core, 1)]
        return 0

    lax.fori_loop(0, LEV, keep, 0)
    for g in range(TR // 8):
        march(core, (g,), range(1, 8), 1, source0, mixes, cm, cp, cd, storing(source1))
        march(core, (g,), range(2, 7), 1, source1, mixes, cm, cp, cd, storing(source2))
        final_step(core, (g,), range(3, 6), 1, source2, mixes, cm, cp, cd, kp, lambda p: triple(core, p - 3), done, prefix)
    copy = pltpu.make_async_copy(done.at[pl.ds(0, LEV)], out.at[:, pl.ds(3 - 3 * core, 3)], sem)
    copy.start()
    transposed_rows(prefix, table, lambda q: q * ROWS)
    copy.wait()


def late_kernel(core_ref, kp, rows, halo, carry, wind, mix, wind_mix_halo, early_table, mask, fields_in, out, jac, faces, mixes, cm, cp, cd, s1, s2, done, prefix, table, picked, sem, table_sem):
    core = core_ref[0]
    table_copy = pltpu.make_async_copy(early_table, table.at[pl.ds((3 - 3 * core) * ROWS, 3 * ROWS)], table_sem)
    table_copy.start()
    faces[3:9, :LEV] = wind[...]
    faces[pl.ds(9 * core, 3), :LEV] = wind_mix_halo[0:3]
    mixes[2:8, :LEV] = mix[...]
    mixes[pl.ds(8 * core, 2), :LEV] = wind_mix_halo[3:5]
    coefficients(core, faces, mixes, range(-2, 3), cm, cp, cd)

    def source0(l, p):
        return (carry, (l, p)) if p >= 0 else (halo, (l, triple(core, p + 3)))

    def source1(l, p):
        return (carry, (l, p + 1)) if p >= 1 else (s1, (l, p + 2))

    def source2(l, p):
        return (carry, (l, p + 2)) if p >= 2 else (s2, (l, p + 1))

    for groups in GROUPS:
        march(core, groups, range(-2, 1), -2, source0, mixes, cm, cp, cd, storing(source1))
        march(core, groups, range(-1, 2), -2, source1, mixes, cm, cp, cd, storing(source2))
        final_step(core, groups, range(0, 3), -2, source2, mixes, cm, cp, cd, kp, lambda p: triple(core, p), done, prefix)
    copy = pltpu.make_async_copy(done.at[pl.ds(0, LEV)], out.at[:, pl.ds(3 * core, 3)], sem)
    copy.start()
    transposed_rows(prefix, table, lambda q: pl.multiple_of((3 * core + q) * ROWS, ROWS))
    table_copy.wait()

    def pick(block, _):
        for u in range(16):
            k = block * 16 + u
            picked[pl.ds(k, 1), :] = table[pl.ds(rows[k], 1), :]
        return 0

    lax.fori_loop(0, OBS // 16, pick, 0)
    kept = jnp.where(mask[...] > 0.5, picked[...], 0.0)
    same = lax.broadcasted_iota(jnp.int32, (TR, 128), 1) % TR == lax.broadcasted_iota(jnp.int32, (TR, 128), 0)
    jac[...] = lax.dot_general(same.astype(F32), kept, (((1,), (1,)), ((), ())), precision=EXACT, preferred_element_type=F32)
    copy.wait()


def gram_kernel(trc_ref, mine, other, weight, innov, out, full, padded):
    trc = trc_ref[0]
    full[pl.ds(pl.multiple_of(trc * TR, TR), TR)] = mine[...]
    full[pl.ds(pl.multiple_of(TR - trc * TR, TR), TR)] = other[...]
    jac = full[...]
    padded[0:32] = jac
    padded[32:128] = jnp.zeros((96, OBS), F32)
    weighted = jac * weight[...]
    both = (((1,), (1,)), ((), ()))
    gram = lax.dot_general(weighted, padded[...], both, precision=EXACT, preferred_element_type=F32)
    lhs = jnp.broadcast_to(weight[...] * innov[...], (8, OBS))
    out[0:8] = sum((pltpu.roll(gram[8 * k : 8 * k + 8], 32 * k, 1) for k in range(1, 4)), gram[0:8])
    out[8:16] = lax.dot_general(lhs, padded[...], both, precision=EXACT, preferred_element_type=F32)


def solve_kernel(total, prior, full, live, innov, update, misfit):
    lane = lax.broadcasted_iota(jnp.int32, (32, 128), 1)
    row = lax.broadcasted_iota(jnp.int32, (32, 128), 0)
    packed = total[0:8]
    gram = jnp.concatenate([packed] + [pltpu.roll(packed, 128 - 32 * k, 1) for k in range(1, 4)], 0)
    diagonal = lane == row
    gram = gram + jnp.where(diagonal, jnp.broadcast_to(prior[...], (32, 128)), 0.0)
    side = jnp.sum(jnp.where(diagonal, jnp.broadcast_to(total[8:9], (32, 128)), 0.0), 1, keepdims=True)
    aug = jnp.where(lane < 32, gram, jnp.where(lane == 32, side, 0.0))
    for k in range(32):
        top = aug[k : k + 1] / aug[k : k + 1, k : k + 1]
        aug = jnp.where(row == k, top, aug - aug[:, k : k + 1] * top)
    answer = aug[:, 32:33]
    update[...] = jnp.sum(jnp.where(diagonal, answer, 0.0), 0)[:32]
    fitted = jnp.sum(full[...] * answer, 0, keepdims=True)
    fitted = jnp.concatenate([fitted[:, 128 * k : 128 * k + 128] for k in range(OBS // 128)], 0)
    misfit[...] = live[...] * (innov[...] - fitted)


def vmem(n):
    return [pl.BlockSpec(memory_space=pltpu.VMEM)] * n


def smem(n):
    return [pl.BlockSpec(memory_space=pltpu.SMEM)] * n


def anywhere(n):
    return [pl.BlockSpec(memory_space=pl.ANY)] * n


def of(*dims):
    return jax.ShapeDtypeStruct(dims, F32)


def work(*dims):
    return pltpu.VMEM(dims, F32)


def kept(*dims):
    return pltpu.VMEM(dims, F32)


def near(*arrays):
    return [pltpu.with_memory_space_constraint(x, pltpu.VMEM) for x in arrays]


def limit(mib):
    return pltpu.CompilerParams(vmem_limit_bytes=mib << 20)


def pairs(remote):
    n = 128
    low = [(i, (i + 1) % n) for i in range(1 if remote else 0, n, 2)]
    return low + [(j, i) for i, j in low]


def stages():
    yield "tile_3", [(i, i ^ 1) for i in range(2)]
    for flip in (1, 3):
        yield "tile_0", [(i, i ^ flip) for i in range(4)]
    for flip in (1, 2, 6):
        yield "tile_2", [(i, i ^ flip) for i in range(8)]
    yield "tile_1", [(i, i ^ 1) for i in range(2)]


def per_device(tracers, courant, vertical_mix, kernel_profile, obs_cell, obs_top, obs_count, innovation, obs_error, prior_precision):
    core = lax.axis_index("tile_3").astype(jnp.int32)
    trc = lax.axis_index("trc").astype(jnp.int32)
    core_at, trc_at = core.reshape(1), trc.reshape(1)
    cells = pltpu.with_memory_space_constraint(jnp.transpose(tracers, (1, 2, 0, 3)), pltpu.HBM)
    wind = jnp.transpose(courant, (1, 0, 2))
    mix = jnp.transpose(vertical_mix, (1, 0, 2))

    def edge(side):
        return pl.pallas_call(
            edge_kernel,
            out_shape=kept(LEV, 3, TR, LAT),
            in_specs=smem(1) + anywhere(1),
            out_specs=vmem(1)[0],
            scratch_shapes=[pltpu.SemaphoreType.DMA((4,))],
            compiler_params=limit(4),
            name="edge",
        )(side.reshape(1), cells)

    def rim(side):
        return jnp.concatenate([lax.dynamic_slice_in_dim(wind, 3 * side, 3, 0), lax.dynamic_slice_in_dim(mix, 4 * side, 2, 0)], 0)

    far_halo = lax.ppermute(edge(core), TILE, pairs(True))
    near_edge = edge(1 - core)
    near_halo = lax.ppermute(near_edge, TILE, pairs(False))
    near_rim = lax.ppermute(rim(1 - core), TILE, pairs(False))
    far_rim = lax.ppermute(rim(core), TILE, pairs(True))

    block = (LEV, 6, TR, LAT)
    profile = jnp.pad(kernel_profile, (0, LEVELS - LEV))
    fields, carry, early_table = pl.pallas_call(
        early_kernel,
        out_shape=(of(*block), kept(LEVELS, 6, TR, LAT), kept(3 * ROWS, 128)),
        in_specs=smem(2) + anywhere(1) + vmem(4),
        out_specs=anywhere(1) + vmem(2),
        scratch_shapes=[work(12, 48, LAT), work(10, 48, LAT), work(LEV, 6, TR, LAT), work(7, 48, LAT), work(7, 48, LAT), work(7, 48, LAT),
                        work(48, 5, TR, LAT), work(48, 3, TR, LAT), work(48, 3, TR, LAT), work(48, 3, TR, LAT), pltpu.SemaphoreType.DMA, pltpu.SemaphoreType.DMA((4,))],
        compiler_params=limit(30),
        cost_estimate=pl.CostEstimate(flops=10**9, transcendentals=0, bytes_accessed=15 * 10**6),
        name="early",
    )(core_at, profile, cells, *near(near_halo, wind, mix, near_rim))

    cell = jnp.clip(obs_cell, 0, 6 * LAT - 1)
    level = jnp.clip(obs_top, 1, LEV) - 1
    rows = (cell // LAT) * ROWS + (level // 8) * LAT + cell % LAT
    lanes = lax.broadcasted_iota(jnp.int32, (OBS, 128), 1) // TR
    mask = (lanes == (level % 8)[:, None]).astype(F32)
    slots = jnp.arange(OBS, dtype=jnp.int32)
    live = (slots < obs_count[0]).astype(F32)
    weight = (live / obs_error).reshape(1, OBS)

    fields, mine = pl.pallas_call(
        late_kernel,
        out_shape=(of(*block), kept(TR, OBS)),
        in_specs=smem(3) + vmem(5) + anywhere(1) + vmem(1) + anywhere(1),
        out_specs=anywhere(1) + vmem(1),
        scratch_shapes=[work(12, 48, LAT), work(10, 48, LAT), work(5, 48, LAT), work(5, 48, LAT), work(5, 48, LAT),
                        work(48, 3, TR, LAT), work(48, 3, TR, LAT), work(48, 3, TR, LAT), work(48, 3, TR, LAT),
                        work(6 * ROWS, 128), work(OBS, 128), pltpu.SemaphoreType.DMA, pltpu.SemaphoreType.DMA],
        input_output_aliases={10: 0},
        compiler_params=limit(34),
        cost_estimate=pl.CostEstimate(flops=10**9, transcendentals=0, bytes_accessed=15 * 10**6),
        name="late",
    )(core_at, profile, rows, *near(far_halo, carry, wind, mix, far_rim, early_table, mask), fields)

    other = lax.ppermute(mine, "trc", [(0, 1), (1, 0)])
    total, full = pl.pallas_call(
        gram_kernel,
        out_shape=(kept(16, 128), kept(2 * TR, OBS)),
        in_specs=smem(1) + vmem(4),
        out_specs=vmem(2),
        scratch_shapes=[work(128, OBS)],
        compiler_params=limit(8),
        name="gram",
    )(trc_at, *near(mine, other, weight, innovation.reshape(1, OBS)))
    for axis, swap in stages():
        total = total + lax.ppermute(total, axis, swap)

    prior = jnp.pad(prior_precision, (0, 96)).reshape(1, 128)
    update, misfit = pl.pallas_call(
        solve_kernel,
        out_shape=(of(32), of(OBS // 128, 128)),
        in_specs=vmem(5),
        out_specs=vmem(2),
        compiler_params=limit(4),
        name="solve",
    )(*near(total, prior, full, live.reshape(OBS // 128, 128), innovation.reshape(OBS // 128, 128)))
    return (jnp.transpose(fields, (2, 0, 1, 3)), update, misfit.reshape(OBS))


def solution(mesh):
    split = Mesh(
        mesh.devices.reshape(4, 2, 8, 2, mesh.shape["trc"]),
        ("tile_0", "tile_1", "tile_2", "tile_3", "trc"),
    )
    return jax.shard_map(
        per_device,
        mesh=split,
        in_specs=(P("trc", None, TILE, None), P(None, TILE, None), P(None, TILE, None), P(), P(TILE), P(TILE), P(TILE), P(TILE), P(TILE), P()),
        out_specs=(P("trc", None, TILE, None), P(), P(TILE)),
        check_vma=False,
    )
```

time: 261 us -> 94.3 us (0.36)
  the two profiles are of different devices: /device:TPU:1 before, /device:TPU:16 now
where the time goes in v1:
time: 94.3 us; the launch traced here: 94 us
  waiting for transfers between devices  41.9 us (44%)
  Pallas kernels  38.1 us (40%)
  starting transfers between devices  12 us (13%)
  between operations  1.51 us (2%)
    ppermute x7, waiting for transfers between devices, per_device(): total = total + lax.ppermute(total, axis, swap)  26.3 us
    pallas_call x1, Pallas kernels, per_device(): pl.pallas_call(early_kernel, out_shape=(of(*block), kept(LEVELS, 6, TR, L...  16.6 us
    pallas_call x1, Pallas kernels, per_device(): pl.pallas_call(late_kernel, out_shape=(of(*block), kept(TR, OBS)), in_spe...  11.3 us
    ppermute x1, waiting for transfers between devices, per_device(): far_rim = lax.ppermute(rim(core), TILE, pairs(True))  9.76 us
    ppermute x1, starting transfers between devices, per_device(): far_halo = lax.ppermute(edge(core), TILE, pairs(True))  8.92 us
    pallas_call x2, Pallas kernels, edge(): pl.pallas_call(edge_kernel, out_shape=kept(LEV, 3, TR, LAT), in_specs=sme...  6.1 us
    ppermute x1, waiting for transfers between devices, per_device(): other = lax.ppermute(mine, 'trc', [(0, 1), (1, 0)])  5.83 us
    pallas_call x1, Pallas kernels, per_device(): pl.pallas_call(solve_kernel, out_shape=(of(32), of(OBS // 128, 128)), in_...  3.49 us
  transfers between devices with their start and end apart: 12, of which 9 were waited for; matrix products, arithmetic and copies ran while one was open for 1% of the time, Pallas kernels for 21%

profile of v1, /device:TPU:16, one launch (start us, length us, event | category | flops | bytes accessed | tf_op | source)
XLA Modules:
  0.0 94.0 jit_solution(7977223815549606595)
XLA Ops:
  0.6 3.0 %edge.3 = f32[47,3,16,256]{3,2,1,0:T(8,128)} custom-call(s32[1]{0:T(128)} %bitcast.2.side_ref, f32[47,6,16,256]{3,2,1,0:T(8,128)} %bitcast.31), custom_call_target="tpu_custom_call" | custom-call | tf_op jit(solution)/shard_map/edge/pallas_call | solution.py:303
  3.6 0.1 collective-permute-start.1
  3.8 0.0 copy-start.1
  3.8 0.0 copy-start
  3.8 0.0 copy-start.4
  3.8 0.0 copy-start.5
  3.8 3.1 %edge.2 = f32[47,3,16,256]{3,2,1,0:T(8,128)} custom-call(s32[1]{0:T(128)} %bitcast.side_ref.core_ref, f32[47,6,16,256]{3,2,1,0:T(8,128)} %bitcast.32), custom_call_target="tpu_custom_call" | custom-call | tf_op jit(solution)/shard_map/edge/pallas_call | solution.py:303
  6.9 0.0 copy-start.6
  6.9 8.9 %collective-permute-start = (f32[47,3,16,256]{3,2,1,0:T(8,128)}, f32[47,3,16,256]{3,2,1,0:T(8,128)}, u32[]{:S(2)}, u32[]{:S(2)}) collective-permute-start(f32[47,3,16,256]{3,2,1,0:T(8,128)} %edge.2), channel_id=1, source_target_pairs={{2,4},{6,8},{10,12},{14,16},{18,20},{22,24},{26,28},{30,32},{34,36... | collective-permute-start | bytes 6930440 | tf_op jit(solution)/shard_map/ppermute | solution.py:316
  15.8 0.0 copy-done.1
  15.9 0.0 copy-done
  15.9 0.1 collective-permute-start.2
  16.1 1.2 %collective-permute-start.3 = (f32[5,47,256]{2,1,0:T(8,128)S(1)}, f32[5,47,256]{2,1,0:T(8,128)S(1)}, u32[]{:S(2)}, u32[]{:S(2)}) collective-permute-start(f32[5,47,256]{2,1,0:T(8,128)S(1)} %pad_maximum_fusion.1), channel_id=1, source_target_pairs={{2,4},{6,8},{10,12},{14,16},{18,20},{22,24},{26,28},{30,32},{34,36... | collective-permute-start | bytes 721928 | tf_op jit(solution)/shard_map/ppermute | solution.py:320
  17.3 0.0 copy-done.4
  17.3 0.0 copy-done.5
  17.3 0.3 fusion.mask
  18.3 0.0 copy-done.6
  18.3 0.0 collective-permute-done.2.wind_mix_halo
  18.3 0.0 collective-permute-done.1.halo
  18.3 16.6 %early.1 = (f32[47,6,16,256]{3,2,1,0:T(8,128)}, f32[48,6,16,256]{3,2,1,0:T(8,128)S(1)}, f32[4608,128]{1,0:T(8,128)S(1)}) custom-call(s32[1]{0:T(128)} %bitcast.side_ref.core_ref, f32[48]{0:T(128)S(1)} %pad.8.kp, f32[47,6,16,256]{3,2,1,0:T(8,128)} %bitcast.33, f32[47,3,16,256]{3,2,1,0:T(8,128)} %collective-permute-done.1.halo, f32[6,47,256]{2,1,0:T(8,128)S(1)} %bitcast.24, ...), custom_call_target="tpu_custom_call" | custom-call | flops 1000000000 | bytes 15000000 | tf_op jit(solution)/shard_map/early/pallas_call | solution.py:324
  34.9 9.8 %collective-permute-done.3.wind_mix_halo = f32[5,47,256]{2,1,0:T(8,128)S(1)} collective-permute-done((f32[5,47,256]{2,1,0:T(8,128)S(1)}, f32[5,47,256]{2,1,0:T(8,128)S(1)}, u32[]{:S(2)}, u32[]{:S(2)}) %collective-permute-start.3) | collective-permute-done | bytes 240672 | tf_op jit(solution)/shard_map/ppermute | solution.py:320
  44.7 0.0 collective-permute-done.halo
  44.7 0.0 copy-start.3
  44.7 0.0 copy-start.2
  44.7 0.0 copy-start.7
  44.7 11.3 %late.1 = (f32[47,6,16,256]{3,2,1,0:T(8,128)}, f32[16,2048]{1,0:T(8,128)S(1)}) custom-call(s32[1]{0:T(128)} %bitcast.side_ref.core_ref, f32[48]{0:T(128)S(1)} %pad.8.kp, s32[2048]{0:T(1024)S(1)} %get-tuple-element.26.rows, f32[47,3,16,256]{3,2,1,0:T(8,128)} %collective-permute-done.halo, ...), custom_call_target="tpu_custom_call", output_to_operand_aliasing={{0}: (10, {})} | custom-call | flops 1000000000 | bytes 15000000 | tf_op jit(solution)/shard_map/late/pallas_call | solution.py:345
  56.0 0.7 collective-permute-start.4
  56.7 0.0 copy-done.3
  56.7 5.8 %collective-permute-done.4.other = f32[16,2048]{1,0:T(8,128)S(1)} collective-permute-done((f32[16,2048]{1,0:T(8,128)S(1)}, f32[16,2048]{1,0:T(8,128)S(1)}, u32[]{:S(2)}, u32[]{:S(2)}) %collective-permute-start.4) | collective-permute-done | bytes 131104 | tf_op jit(solution)/shard_map/ppermute | solution.py:359
  62.6 0.0 copy-done.2
  62.6 0.6 gram.1
  63.2 0.0 collective-permute-start.5
  63.2 1.2 %collective-permute-done.5 = f32[16,128]{1,0:T(8,128)S(1)} collective-permute-done((f32[16,128]{1,0:T(8,128)S(1)}, f32[16,128]{1,0:T(8,128)S(1)}, u32[]{:S(2)}, u32[]{:S(2)}) %collective-permute-start.5) | collective-permute-done | bytes 8224 | tf_op jit(solution)/shard_map/ppermute | solution.py:370
  64.4 0.0 collective-permute-start.6
  64.4 3.6 %collective-permute-done.6 = f32[16,128]{1,0:T(8,128)S(1)} collective-permute-done((f32[16,128]{1,0:T(8,128)S(1)}, f32[16,128]{1,0:T(8,128)S(1)}, u32[]{:S(2)}, u32[]{:S(2)}) %collective-permute-start.6) | collective-permute-done | bytes 8224 | tf_op jit(solution)/shard_map/ppermute | solution.py:370
  68.1 0.8 collective-permute-start.7
  68.9 4.0 %collective-permute-done.7 = f32[16,128]{1,0:T(8,128)S(1)} collective-permute-done((f32[16,128]{1,0:T(8,128)S(1)}, f32[16,128]{1,0:T(8,128)S(1)}, u32[]{:S(2)}, u32[]{:S(2)}) %collective-permute-start.7) | collective-permute-done | bytes 8224 | tf_op jit(solution)/shard_map/ppermute | solution.py:370
  72.9 0.0 collective-permute-start.8
  72.9 3.6 %collective-permute-done.8 = f32[16,128]{1,0:T(8,128)S(1)} collective-permute-done((f32[16,128]{1,0:T(8,128)S(1)}, f32[16,128]{1,0:T(8,128)S(1)}, u32[]{:S(2)}, u32[]{:S(2)}) %collective-permute-start.8) | collective-permute-done | bytes 8224 | tf_op jit(solution)/shard_map/ppermute | solution.py:370
  76.6 0.0 collective-permute-start.9
  76.6 4.5 %collective-permute-done.9 = f32[16,128]{1,0:T(8,128)S(1)} collective-permute-done((f32[16,128]{1,0:T(8,128)S(1)}, f32[16,128]{1,0:T(8,128)S(1)}, u32[]{:S(2)}, u32[]{:S(2)}) %collective-permute-start.9) | collective-permute-done | bytes 8224 | tf_op jit(solution)/shard_map/ppermute | solution.py:370
  81.1 0.1 collective-permute-start.10
  81.2 5.7 %collective-permute-done.10 = f32[16,128]{1,0:T(8,128)S(1)} collective-permute-done((f32[16,128]{1,0:T(8,128)S(1)}, f32[16,128]{1,0:T(8,128)S(1)}, u32[]{:S(2)}, u32[]{:S(2)}) %collective-permute-start.10) | collective-permute-done | bytes 8224 | tf_op jit(solution)/shard_map/ppermute | solution.py:370
  86.9 0.0 collective-permute-start.11
  86.9 0.0 copy-done.7
  86.9 3.6 %collective-permute-done.11 = f32[16,128]{1,0:T(8,128)S(1)} collective-permute-done((f32[16,128]{1,0:T(8,128)S(1)}, f32[16,128]{1,0:T(8,128)S(1)}, u32[]{:S(2)}, u32[]{:S(2)}) %collective-permute-start.11) | collective-permute-done | bytes 8224 | tf_op jit(solution)/shard_map/ppermute | solution.py:370
  90.5 3.5 %solve.1 = (f32[32]{0:T(128)}, f32[16,128]{1,0:T(8,128)}) custom-call(f32[16,128]{1,0:T(8,128)S(1)} %add.73.total, f32[1,128]{1,0:T(1,128)S(1)} %pad_bitcast_fusion.prior, f32[32,2048]{1,0:T(8,128)S(1)} %get-tuple-element.18.full, f32[16,128]{1,0:T(8,128)S(1)} %fusion.7.live, f32[16,128]{1,0:T(8,128)S(1)} %bitcast.29), custom_call_target="tpu_custom_call" | custom-call | tf_op jit(solution)/shard_map/solve/pallas_call | solution.py:373
  (18 shorter events, 0.2 us)
Async XLA Ops:
  3.6 14.7 %collective-permute-start.1 = (f32[47,3,16,256]{3,2,1,0:T(8,128)}, f32[47,3,16,256]{3,2,1,0:T(8,128)}, u32[]{:S(2)}, u32[]{:S(2)}) collective-permute-start(f32[47,3,16,256]{3,2,1,0:T(8,128)} %edge.3), channel_id=1, source_target_pairs={{0,2},{4,6},{8,10},{12,14},{16,18},{20,22},{24,26},{28,30},{32,34}... | collective-permute-start | bytes 6930440 | tf_op jit(solution)/shard_map/ppermute | solution.py:318
  3.8 12.1 %copy-start.1 = (f32[47,6,256]{2,0,1:T(8,128)S(1)}, f32[47,6,256]{2,0,1:T(8,128)}, u32[]{:S(2)}) copy-start(f32[47,6,256]{2,0,1:T(8,128)} %param.12) | copy-start | bytes 866308
  3.8 12.1 %copy-start = (f32[47,6,256]{2,0,1:T(8,128)S(1)}, f32[47,6,256]{2,0,1:T(8,128)}, u32[]{:S(2)}) copy-start(f32[47,6,256]{2,0,1:T(8,128)} %param.11) | copy-start | bytes 866308
  3.8 13.5 %copy-start.4 = (s32[2048]{0:T(1024)S(1)}, s32[2048]{0:T(1024)}, u32[]{:S(2)}) copy-start(s32[2048]{0:T(1024)} %param.15) | copy-start | bytes 24580
  3.8 13.5 %copy-start.5 = (s32[2048]{0:T(1024)S(1)}, s32[2048]{0:T(1024)}, u32[]{:S(2)}) copy-start(s32[2048]{0:T(1024)} %param.14) | copy-start | bytes 24580
  6.9 11.4 %copy-start.6 = (f32[47]{0:T(128)S(1)}, f32[47]{0:T(128)}, u32[]{:S(2)}) copy-start(f32[47]{0:T(128)} %param.13) | copy-start | bytes 568
  6.9 37.8 %collective-permute-start = (f32[47,3,16,256]{3,2,1,0:T(8,128)}, f32[47,3,16,256]{3,2,1,0:T(8,128)}, u32[]{:S(2)}, u32[]{:S(2)}) collective-permute-start(f32[47,3,16,256]{3,2,1,0:T(8,128)} %edge.2), channel_id=1, source_target_pairs={{2,4},{6,8},{10,12},{14,16},{18,20},{22,24},{26,28},{30,32},{34,36... | collective-permute-start | bytes 6930440 | tf_op jit(solution)/shard_map/ppermute | solution.py:316
  15.9 2.4 %collective-permute-start.2 = (f32[5,47,256]{2,1,0:T(8,128)S(1)}, f32[5,47,256]{2,1,0:T(8,128)S(1)}, u32[]{:S(2)}, u32[]{:S(2)}) collective-permute-start(f32[5,47,256]{2,1,0:T(8,128)S(1)} %pad_maximum_fusion), channel_id=1, source_target_pairs={{0,2},{4,6},{8,10},{12,14},{16,18},{20,22},{24,26},{28,30},{32,34}... | collective-permute-start | bytes 721928 | tf_op jit(solution)/shard_map/ppermute | solution.py:319
  16.1 28.6 %collective-permute-start.3 = (f32[5,47,256]{2,1,0:T(8,128)S(1)}, f32[5,47,256]{2,1,0:T(8,128)S(1)}, u32[]{:S(2)}, u32[]{:S(2)}) collective-permute-start(f32[5,47,256]{2,1,0:T(8,128)S(1)} %pad_maximum_fusion.1), channel_id=1, source_target_pairs={{2,4},{6,8},{10,12},{14,16},{18,20},{22,24},{26,28},{30,32},{34,36... | collective-permute-start | bytes 721928 | tf_op jit(solution)/shard_map/ppermute | solution.py:320
  44.7 12.0 %copy-start.3 = (f32[2048]{0:T(1024)S(1)}, f32[2048]{0:T(1024)}, u32[]{:S(2)}) copy-start(f32[2048]{0:T(1024)} %param.18) | copy-start | bytes 24580
  44.7 17.9 %copy-start.2 = (f32[2048]{0:T(1024)S(1)}, f32[2048]{0:T(1024)}, u32[]{:S(2)}) copy-start(f32[2048]{0:T(1024)} %param.17) | copy-start | bytes 24580
  44.7 42.2 %copy-start.7 = (f32[32]{0:T(128)S(1)}, f32[32]{0:T(128)}, u32[]{:S(2)}) copy-start(f32[32]{0:T(128)} %param.19) | copy-start | bytes 388
  56.0 6.6 %collective-permute-start.4 = (f32[16,2048]{1,0:T(8,128)S(1)}, f32[16,2048]{1,0:T(8,128)S(1)}, u32[]{:S(2)}, u32[]{:S(2)}) collective-permute-start(f32[16,2048]{1,0:T(8,128)S(1)} %get-tuple-element.16.mine), channel_id=1, source_target_pairs={{0,1},{1,0},{2,3},{3,2},{4,5},{5,4},{6,7},{7,6},{8,9},{9,8},{10,11... | collective-permute-start | bytes 393224 | tf_op jit(solution)/shard_map/ppermute | solution.py:359
  63.2 1.2 %collective-permute-start.5 = (f32[16,128]{1,0:T(8,128)S(1)}, f32[16,128]{1,0:T(8,128)S(1)}, u32[]{:S(2)}, u32[]{:S(2)}) collective-permute-start(f32[16,128]{1,0:T(8,128)S(1)} %get-tuple-element.17), channel_id=1, source_target_pairs={{0,2},{2,0},{1,3},{3,1},{4,6},{6,4},{5,7},{7,5},{8,10},{10,8},{9,1... | collective-permute-start | bytes 24584 | tf_op jit(solution)/shard_map/ppermute | solution.py:370
  64.4 3.7 %collective-permute-start.6 = (f32[16,128]{1,0:T(8,128)S(1)}, f32[16,128]{1,0:T(8,128)S(1)}, u32[]{:S(2)}, u32[]{:S(2)}) collective-permute-start(f32[16,128]{1,0:T(8,128)S(1)} %add.67), channel_id=1, source_target_pairs={{0,64},{64,0},{128,192},{192,128},{1,65},{65,1},{129,193},{193,129... | collective-permute-start | bytes 24584 | tf_op jit(solution)/shard_map/ppermute | solution.py:370
  68.1 4.9 %collective-permute-start.7 = (f32[16,128]{1,0:T(8,128)S(1)}, f32[16,128]{1,0:T(8,128)S(1)}, u32[]{:S(2)}, u32[]{:S(2)}) collective-permute-start(f32[16,128]{1,0:T(8,128)S(1)} %add.68), channel_id=1, source_target_pairs={{0,192},{64,128},{128,64},{192,0},{1,193},{65,129},{129,65},{193,1... | collective-permute-start | bytes 24584 | tf_op jit(solution)/shard_map/ppermute | solution.py:370
  72.9 3.7 %collective-permute-start.8 = (f32[16,128]{1,0:T(8,128)S(1)}, f32[16,128]{1,0:T(8,128)S(1)}, u32[]{:S(2)}, u32[]{:S(2)}) collective-permute-start(f32[16,128]{1,0:T(8,128)S(1)} %add.69), channel_id=1, source_target_pairs={{0,4},{4,0},{8,12},{12,8},{16,20},{20,16},{24,28},{28,24},{1,5},{5... | collective-permute-start | bytes 24584 | tf_op jit(solution)/shard_map/ppermute | solution.py:370
  76.6 4.5 %collective-permute-start.9 = (f32[16,128]{1,0:T(8,128)S(1)}, f32[16,128]{1,0:T(8,128)S(1)}, u32[]{:S(2)}, u32[]{:S(2)}) collective-permute-start(f32[16,128]{1,0:T(8,128)S(1)} %add.70), channel_id=1, source_target_pairs={{0,8},{4,12},{8,0},{12,4},{16,24},{20,28},{24,16},{28,20},{1,9},{5... | collective-permute-start | bytes 24584 | tf_op jit(solution)/shard_map/ppermute | solution.py:370
  81.1 5.8 %collective-permute-start.10 = (f32[16,128]{1,0:T(8,128)S(1)}, f32[16,128]{1,0:T(8,128)S(1)}, u32[]{:S(2)}, u32[]{:S(2)}) collective-permute-start(f32[16,128]{1,0:T(8,128)S(1)} %add.71), channel_id=1, source_target_pairs={{0,24},{4,28},{8,16},{12,20},{16,8},{20,12},{24,0},{28,4},{1,25},{... | collective-permute-start | bytes 24584 | tf_op jit(solution)/shard_map/ppermute | solution.py:370
  86.9 3.7 %collective-permute-start.11 = (f32[16,128]{1,0:T(8,128)S(1)}, f32[16,128]{1,0:T(8,128)S(1)}, u32[]{:S(2)}, u32[]{:S(2)}) collective-permute-start(f32[16,128]{1,0:T(8,128)S(1)} %add.72), channel_id=1, source_target_pairs={{0,32},{32,0},{1,33},{33,1},{2,34},{34,2},{3,35},{35,3},{4,36},{36... | collective-permute-start | bytes 24584 | tf_op jit(solution)/shard_map/ppermute | solution.py:370
